TPU v7x, 16 devices: a 4x2x1 block of a 4x4x8 slice. The times are simulated.
16 devices in a mesh: dp: 4 (over y, z, core), tp: 4 (over x).
Axes of the slice: x: 4, y: 2, z: 1, core: 2. Of those that a mesh axis runs over, the one named last changes fastest.
The devices are a block of a 4x4x8 slice.
Arguments:
- x: bfloat16 [512, 5120], P('dp'), parts along dimension 0
- w_gate: bfloat16 [5120, 25600], P(None, 'tp')
- w_up: bfloat16 [5120, 25600], P(None, 'tp')
- w_down: bfloat16 [25600, 5120], P('tp')
Outputs:
- output: bfloat16 [512, 5120], P('dp'), parts along dimension 0
There are 4 independent parts. A program takes and returns all parts, laid end to end along the dimension named above; an argument that names none is the same for every part.
All inputs are finite; a program needn't handle non-finite values.
Results may differ from a plain program's by a relative error of at most 0.016.
Values are sent between devices in bfloat16 or wider.
A program may use at most 768 MiB of HBM per device.

v0:
```python
import jax
import jax.numpy as jnp
from jax import lax
from jax.sharding import PartitionSpec as P


def solution(mesh):
    def step(x, w_gate, w_up, w_down):
        gate = jnp.dot(x, w_gate, preferred_element_type=jnp.float32)
        up = jnp.dot(x, w_up, preferred_element_type=jnp.float32)
        hidden = (jax.nn.silu(gate) * up).astype(jnp.bfloat16)
        term = jnp.dot(hidden, w_down, preferred_element_type=jnp.float32).astype(jnp.bfloat16)
        return lax.psum(term, "tp")

    return jax.shard_map(
        step,
        mesh=mesh,
        in_specs=(P("dp", None), P(None, "tp"), P(None, "tp"), P("tp", None)),
        out_specs=P("dp", None),
        check_vma=False,
    )
```

profile of v0, /device:TPU:112, one launch (start us, length us, event | category | flops | bytes accessed | tf_op | source)
XLA Modules:
  0.0 132.4 jit_solution(2892273077427944587)
XLA Ops:
  6.5 0.0 copy-start
  6.6 0.0 all-reduce.2.cloned.1.call-start
  6.6 1.3 copy-done
  7.9 23.9 %fusion.8 = f32[128,6400]{1,0:T(8,128)} fusion(bf16[128,5120]{1,0:T(8,128)(2,1)S(1)} %copy-done, bf16[5120,6400]{1,0:T(8,128)(2,1)} %param.5), kind=kOutput, calls=%fused_computation.10 | convolution fusion | flops 8388608000 | bytes 70123520 | tf_op jit(solution)/shard_map/dot_general | solution.py:9
  31.8 24.1 %fusion.clone.4 = bf16[128,6400]{1,0:T(8,128)(2,1)S(1)} fusion(bf16[128,5120]{1,0:T(8,128)(2,1)S(1)} %copy-done, bf16[5120,6400]{1,0:T(8,128)(2,1)} %param.6, f32[128,6400]{1,0:T(8,128)} %fusion.8), kind=kOutput, calls=%fused_computation.1.clone.clone.clone.1 | convolution fusion | flops 8393523200 | bytes 71761920 | tf_op jit(solution)/shard_map/dot_general | solution.py:10
  55.9 0.0 copy-start.1
  55.9 24.6 %convolution_convert_fusion = bf16[128,5120]{1,0:T(8,128)(2,1)} fusion(bf16[6400,5120]{1,0:T(8,128)(2,1)} %param.7, bf16[128,6400]{1,0:T(8,128)(2,1)S(1)} %fusion.clone.4), kind=kOutput, calls=%fused_computation.2 | convolution fusion | flops 8389263360 | bytes 68485120 | tf_op jit(solution)/shard_map/dot_general | solution.py:12
  80.5 0.1 all-reduce.2.cloned.1.call-update
  80.6 42.5 %all-reduce.2.cloned.1.call-done = bf16[128,5120]{1,0:T(8,128)(2,1)} async-done(((bf16[128,5120]{1,0:T(8,128)(2,1)}), bf16[128,5120]{1,0:T(8,128)(2,1)}) %all-reduce.2.cloned.1.call-update) | async-done | bytes 1310736 | tf_op jit(solution)/shard_map/psum | solution.py:13
  123.1 2.5 %copy.6 = bf16[128,5120]{1,0:T(8,128)(2,1)} copy(bf16[128,5120]{1,0:T(8,128)(2,1)} %all-reduce.2.cloned.1.call-done) | data formatting | bytes 2621440
  125.6 0.0 copy-done.1
Async XLA Ops:
  6.5 1.3 copy-start
  6.6 116.6 %all-reduce.2.cloned.1.call-start = ((), (), s32[]{:S(2)}) async-start(), calls=%async_computation | async-start | bytes 2621440 | tf_op jit(solution)/shard_map/psum | solution.py:13
  55.9 69.7 %copy-start.1 = (bf16[128,5120]{1,0:T(8,128)(2,1)S(1)}, bf16[128,5120]{1,0:T(8,128)(2,1)}, u32[]{:S(2)}) copy-start(bf16[128,5120]{1,0:T(8,128)(2,1)} %param.4) | copy-start | bytes 3932164
Sparse Core Ops, SparseCore 0:
  80.7 42.3 all-reduce.1
where the time goes:
time: 133 us; the launch traced here: 132 us
  matrix products  72.6 us (55%)
  waiting for transfers between devices  42.6 us (32%)
  between operations  13.4 us (10%)
  local copies, waits for them, and re-layouts  3.78 us (3%)
    psum x1, waiting for transfers between devices, step(): return lax.psum(term, 'tp')  42.5 us
    dot_general x1, matrix products, step(): jnp.dot(hidden, w_down, preferred_element_type=jnp.float32)  24.6 us
    dot_general x1, matrix products, step(): up = jnp.dot(x, w_up, preferred_element_type=jnp.float32)  24.1 us
    dot_general x1, matrix products, step(): gate = jnp.dot(x, w_gate, preferred_element_type=jnp.float32)  23.9 us
    unnamed x5, local copies, waits for them, and re-layouts  3.78 us
  transfers between devices with their start and end apart: 1, of which 1 were waited for; matrix products, arithmetic and copies ran while one was open for 0% of the time, Pallas kernels for 0%

commit v1 on v0

v1 whole, which is shorter than its diff:
```python
import functools

import jax
import jax.numpy as jnp
from jax import lax
from jax.experimental import pallas as pl
from jax.experimental.pallas import tpu as pltpu
from jax.sharding import PartitionSpec as P

MESH = pl.DeviceIdType.MESH
SLOTS = 8
WIDE = 512
XCUT = 4


def kernel(x, wg, wu, wd, y, xs, h, slots, acc, dsend, drecv, term, s1, r1, s2, r2, wsem, xsem, dsem, rsem, gsem):
    rows, d = x.shape
    half = wg.shape[1] // 2
    unit = WIDE // 2
    first = half % unit
    steps = half // unit + 1
    chunks = d // WIDE
    piece = WIDE // 4
    top = rows // 2

    dp, tp = lax.axis_index("dp"), lax.axis_index("tp")
    core = lax.rem(dp, 2)
    other = {"dp": dp + 1 - 2 * core}
    right_at, left_at, far_at = lax.rem(tp + 1, 4), lax.rem(tp + 3, 4), lax.rem(tp + 2, 4)
    right, left = {"tp": right_at}, {"tp": left_at}
    base = core * half

    def gate_up(step, width):
        slot = lax.rem(step, SLOTS)
        at = base if width == first else base + first + (step - 1) * unit
        cols = pl.ds(pl.multiple_of(at, 128), width)
        return [
            pltpu.make_async_copy(w.at[:, cols], slots.at[slot, :, pl.ds(k * width, width)], wsem.at[slot, k])
            for k, w in enumerate((wg, wu))
        ]

    def down(chunk):
        slot = lax.rem(chunk + steps, SLOTS)
        cols = pl.ds(pl.multiple_of(chunk * WIDE, 128), WIDE)
        return pltpu.make_async_copy(
            wd.at[pl.ds(pl.multiple_of(base, 128), half), cols], slots.at[slot, pl.ds(0, half), :], wsem.at[slot, 0]
        )

    def refill(step):
        @pl.when(step < steps)
        def _():
            for c in gate_up(step, unit):
                c.start()

        @pl.when(jnp.logical_and(step >= steps, step < steps + chunks))
        def _():
            down(step - steps).start()

    xw = d // XCUT

    def x_in(k):
        cols = pl.ds(k * xw, xw)
        return pltpu.make_async_copy(x.at[:, cols], xs.at[pl.ds(0, rows), cols], xsem.at[0, k])

    def x_out(k):
        cols = pl.ds(k * xw, xw)
        return pltpu.make_async_remote_copy(
            src_ref=xs.at[pl.ds(0, rows), cols],
            dst_ref=xs.at[pl.ds(rows, rows), cols],
            send_sem=xsem.at[1, k],
            recv_sem=xsem.at[2, k],
            device_id=other,
            device_id_type=MESH,
        )

    for k in range(XCUT):
        x_in(k).start()
    for c in gate_up(0, first):
        c.start()
    for s in range(1, SLOTS):
        for c in gate_up(s, unit):
            c.start()

    barrier = pltpu.get_barrier_semaphore()
    for who in (other, right, left):
        pl.semaphore_signal(barrier, inc=1, device_id=who, device_id_type=MESH)
    pl.semaphore_wait(barrier, 3)

    for k in range(XCUT):
        x_in(k).wait()
        x_out(k).start()
    for k in range(XCUT):
        x_out(k).wait_recv()

    def hidden(step, width, at):
        slot = lax.rem(step, SLOTS)
        for c in gate_up(step, width):
            c.wait()
        both = jnp.dot(xs[...], slots[slot, :, : 2 * width], preferred_element_type=jnp.float32)
        h[:, pl.ds(at, width)] = (jax.nn.silu(both[:, :width]) * both[:, width:]).astype(h.dtype)
        refill(step + SLOTS)

    hidden(0, first, 0)

    @pl.loop(1, steps)
    def _(s):
        hidden(s, unit, pl.multiple_of(first + (s - 1) * unit, 128))

    def send(src, dst, sems, k, j, who):
        return pltpu.make_async_remote_copy(
            src_ref=src, dst_ref=dst, send_sem=sems.at[0, k, j], recv_sem=sems.at[1, k, j], device_id=who, device_id_type=MESH
        )

    def die(j):
        return send(dsend.at[j], drecv.at[j], dsem, 0, j, other)

    def rs1(j, k):
        return send(s1.at[k, j], r1.at[k, j], rsem, k, j, (right, left)[k])

    def rs2(j, k):
        return send(s2.at[k, j], r2.at[k, j], rsem, 2 + k, j, (right, left)[k])

    def block(j, at, k=None):
        span = pl.ds(0, rows) if k is None else pl.ds(k * top, top)
        return y.at[span, pl.ds(pl.multiple_of(j * WIDE + at * piece, 128), piece)]

    def ag1(j, k):
        return send(block(j, tp), block(j, tp), gsem, k, j, (right, left)[k])

    def ag1_in(j, k):
        at = (left_at, right_at)[k]
        return send(block(j, at), block(j, at), gsem, k, j, (right, left)[k])

    def ag2(j, k):
        at = (left_at, right_at)[k]
        return send(block(j, at, k), block(j, at, k), gsem, 2 + k, j, (right, left)[k])

    def ag2_in(j, k):
        return send(block(j, far_at, k), block(j, far_at, k), gsem, 2 + k, j, (right, left)[k])

    def part(j, at, k):
        return term[j, pl.ds(k * top, top), pl.ds(pl.multiple_of(at * piece, 128), piece)]

    def chip_sum(j):
        die(j).wait_recv()
        term[j] = acc[lax.rem(j, 2)] + drecv[j].astype(jnp.float32)
        for k in range(2):
            s1[k, j, 0] = part(j, far_at, k).astype(s1.dtype)
            s1[k, j, 1] = part(j, (right_at, left_at)[k], 1 - k).astype(s1.dtype)
            rs1(j, k).start()

    def pass_on(j):
        for k in range(2):
            rs1(j, k).wait_recv()
            s2[k, j] = (part(j, (right_at, left_at)[k], k) + r1[k, j, 0].astype(jnp.float32)).astype(s2.dtype)
            rs2(j, k).start()

    def finish(j):
        for k in range(2):
            rs2(j, k).wait_recv()
            total = part(j, tp, k) + r2[k, j].astype(jnp.float32) + r1[1 - k, j, 1].astype(jnp.float32)
            block(j, tp, k)[...] = total.astype(y.dtype)
        for k in range(2):
            ag1(j, k).start()

    def forward(j):
        for k in range(2):
            ag1_in(j, k).wait_recv()
            ag2(j, k).start()

    @pl.loop(0, chunks)
    def _(j):
        slot = lax.rem(j + steps, SLOTS)
        down(j).wait()
        out = jnp.dot(h[...], slots[slot, :half, :], preferred_element_type=jnp.float32)
        acc[lax.rem(j, 2)] = out[:rows]
        dsend[j] = out[rows:].astype(dsend.dtype)
        die(j).start()
        refill(j + steps + SLOTS)

        @pl.when(j >= 1)
        def _():
            chip_sum(j - 1)

        @pl.when(j >= 2)
        def _():
            pass_on(j - 2)

    chip_sum(chunks - 1)
    pass_on(chunks - 2)
    pass_on(chunks - 1)

    @pl.loop(0, chunks)
    def _(j):
        finish(j)

    @pl.loop(0, chunks)
    def _(j):
        forward(j)

    @pl.loop(0, chunks)
    def _(j):
        for k in range(2):
            ag2_in(j, k).wait_recv()

    for k in range(XCUT):
        x_out(k).wait_send()

    @pl.loop(0, chunks)
    def _(j):
        die(j).wait_send()
        for k in range(2):
            rs1(j, k).wait_send()
            rs2(j, k).wait_send()
            ag1(j, k).wait_send()
            ag2(j, k).wait_send()


def solution(mesh):
    assert mesh.shape["tp"] == 4 and mesh.shape["dp"] % 2 == 0

    def step(x, w_gate, w_up, w_down):
        rows, d = x.shape
        half = w_gate.shape[1] // 2
        chunks, piece, top = d // WIDE, WIDE // 4, rows // 2
        dma = pltpu.SemaphoreType.DMA
        return pl.pallas_call(
            kernel,
            out_shape=jax.ShapeDtypeStruct((rows, d), jnp.bfloat16),
            in_specs=[pl.BlockSpec(memory_space=pl.ANY)] * 4,
            out_specs=pl.BlockSpec(memory_space=pltpu.VMEM),
            scratch_shapes=[
                pltpu.VMEM((2 * rows, d), jnp.bfloat16),
                pltpu.VMEM((2 * rows, half), jnp.bfloat16),
                pltpu.VMEM((SLOTS, d, WIDE), jnp.bfloat16),
                pltpu.VMEM((2, rows, WIDE), jnp.float32),
                pltpu.VMEM((chunks, rows, WIDE), jnp.bfloat16),
                pltpu.VMEM((chunks, rows, WIDE), jnp.bfloat16),
                pltpu.VMEM((chunks, rows, WIDE), jnp.float32),
                pltpu.VMEM((2, chunks, 2, top, piece), jnp.bfloat16),
                pltpu.VMEM((2, chunks, 2, top, piece), jnp.bfloat16),
                pltpu.VMEM((2, chunks, top, piece), jnp.bfloat16),
                pltpu.VMEM((2, chunks, top, piece), jnp.bfloat16),
                dma((SLOTS, 2)),
                dma((3, XCUT)),
                dma((2, 1, chunks)),
                dma((2, 4, chunks)),
                dma((2, 4, chunks)),
            ],
            compiler_params=pltpu.CompilerParams(
                collective_id=0, has_side_effects=True, vmem_limit_bytes=67043328
            ),
        )(x, w_gate, w_up, w_down)

    return jax.shard_map(
        step,
        mesh=mesh,
        in_specs=(P("dp", None), P(None, "tp"), P(None, "tp"), P("tp", None)),
        out_specs=P("dp", None),
        check_vma=False,
    )
```

time: 133 us -> 78.8 us (0.59)
  Pallas kernels: 0 us -> 76.2 us
  matrix products: 72.6 us -> 0 us
  waiting for transfers between devices: 42.6 us -> 0 us
  between operations: 13.4 us -> 0.01 us
    pallas_call x0 -> x1, Pallas kernels: none -> 76.2 us  [step(): pl.pallas_call(kernel, out_shape=jax.ShapeDtypeStruct((rows, d), jnp.bflo...]
    dot_general x3 -> x0, matrix products: 72.6 us -> none  [the longest x1 24.6 us: step(): jnp.dot(hidden, w_down, preferred_element_type=jnp.float32)]
    psum x1 -> x0, waiting for transfers between devices: 42.5 us -> none  [step(): return lax.psum(term, 'tp')]
    unnamed x5 -> x1, local copies, waits for them, and re-layouts: 3.78 us -> 2.46 us
  transfers between devices with their start and end apart: 1 -> 0, of which waited for: 1 -> 0; matrix products, arithmetic and copies ran while one was open for 0% -> 0% of each run, Pallas kernels for 0% -> 0%
where the time goes in v1:
time: 78.8 us; the launch traced here: 78.7 us
  Pallas kernels  76.2 us (97%)
  local copies, waits for them, and re-layouts  2.46 us (3%)
    pallas_call x1, Pallas kernels, step(): pl.pallas_call(kernel, out_shape=jax.ShapeDtypeStruct((rows, d), jnp.bflo...  76.2 us
    unnamed x1, local copies, waits for them, and re-layouts  2.46 us

profile of v1, /device:TPU:112, one launch (start us, length us, event | category | flops | bytes accessed | tf_op | source)
XLA Modules:
  0.0 78.7 jit_solution(14280495774098440038)
XLA Ops:
  0.0 76.2 %shard_map.46 = bf16[128,5120]{1,0:T(8,128)(2,1)} custom-call(bf16[128,5120]{1,0:T(8,128)(2,1)} %x.1, bf16[5120,6400]{1,0:T(8,128)(2,1)} %wg.1, bf16[5120,6400]{1,0:T(8,128)(2,1)} %wu.1, bf16[6400,5120]{1,0:T(8,128)(2,1)} %wd.1), custom_call_target="tpu_custom_call" | custom-call | tf_op jit(solution)/shard_map/pallas_call | solution.py:227
  76.2 2.5 %copy.6 = bf16[128,5120]{1,0:T(8,128)(2,1)} copy(bf16[128,5120]{1,0:T(8,128)(2,1)} %shard_map.46) | data formatting | bytes 2621440

commit v2 on v1

--- a/solution.py
+++ b/solution.py
@@ -11,6 +11,8 @@
 SLOTS = 8
 WIDE = 512
 XCUT = 4
+EARLY = 2
+LAG = 4
 
 
 def kernel(x, wg, wu, wd, y, xs, h, slots, acc, dsend, drecv, term, s1, r1, s2, r2, wsem, xsem, dsem, rsem, gsem):
@@ -73,22 +75,22 @@
             device_id_type=MESH,
         )
 
-    for k in range(XCUT):
-        x_in(k).start()
-    for c in gate_up(0, first):
-        c.start()
-    for s in range(1, SLOTS):
-        for c in gate_up(s, unit):
-            c.start()
-
     barrier = pltpu.get_barrier_semaphore()
     for who in (other, right, left):
         pl.semaphore_signal(barrier, inc=1, device_id=who, device_id_type=MESH)
+    for k in range(XCUT):
+        x_in(k).start()
+    for s in range(EARLY):
+        for c in gate_up(s, unit if s else first):
+            c.start()
     pl.semaphore_wait(barrier, 3)
 
     for k in range(XCUT):
         x_in(k).wait()
         x_out(k).start()
+    for s in range(EARLY, SLOTS):
+        for c in gate_up(s, unit):
+            c.start()
     for k in range(XCUT):
         x_out(k).wait_recv()
 
@@ -182,13 +184,15 @@
         def _():
             chip_sum(j - 1)
 
-        @pl.when(j >= 2)
-        def _():
-            pass_on(j - 2)
+        @pl.when(j >= LAG)
+        def _():
+            pass_on(j - LAG)
 
     chip_sum(chunks - 1)
-    pass_on(chunks - 2)
-    pass_on(chunks - 1)
+
+    @pl.loop(chunks - LAG, chunks)
+    def _(j):
+        pass_on(j)
 
     @pl.loop(0, chunks)
     def _(j):
@@ -226,7 +230,7 @@
         dma = pltpu.SemaphoreType.DMA
         return pl.pallas_call(
             kernel,
-            out_shape=jax.ShapeDtypeStruct((rows, d), jnp.bfloat16),
+            out_shape=pltpu.VMEM((rows, d), jnp.bfloat16),
             in_specs=[pl.BlockSpec(memory_space=pl.ANY)] * 4,
             out_specs=pl.BlockSpec(memory_space=pltpu.VMEM),
             scratch_shapes=[
@@ -248,7 +252,7 @@
                 dma((2, 4, chunks)),
             ],
             compiler_params=pltpu.CompilerParams(
-                collective_id=0, has_side_effects=True, vmem_limit_bytes=67043328
+                collective_id=0, has_side_effects=True, vmem_limit_bytes=64_000_000
             ),
         )(x, w_gate, w_up, w_down)
 

time: 78.8 us -> 58.6 us (0.74)
  Pallas kernels: 76.2 us -> 57.5 us
  local copies, waits for them, and re-layouts: 2.46 us -> 1.06 us
    pallas_call x1, Pallas kernels: 76.2 us -> 57.5 us  [step(): pl.pallas_call(kernel, out_shape=pltpu.VMEM((rows, d), jnp.bfloat16), in_...]
    unnamed x1, local copies, waits for them, and re-layouts: 2.46 us -> 1.06 us
where the time goes in v2:
time: 58.6 us
  Pallas kernels  57.5 us (98%)
  local copies, waits for them, and re-layouts  1.06 us (2%)
    pallas_call x1, Pallas kernels, step(): pl.pallas_call(kernel, out_shape=pltpu.VMEM((rows, d), jnp.bfloat16), in_...  57.5 us

profile of v2, /device:TPU:112, one launch (start us, length us, event | category | flops | bytes accessed | tf_op | source)
XLA Modules:
  0.0 58.6 jit_solution(15901180336276566341)
XLA Ops:
  0.0 57.5 %shard_map.46 = bf16[128,5120]{1,0:T(8,128)(2,1)S(1)} custom-call(bf16[128,5120]{1,0:T(8,128)(2,1)} %x.1, bf16[5120,6400]{1,0:T(8,128)(2,1)} %wg.1, bf16[5120,6400]{1,0:T(8,128)(2,1)} %wu.1, bf16[6400,5120]{1,0:T(8,128)(2,1)} %wd.1), custom_call_target="tpu_custom_call" | custom-call | tf_op jit(solution)/shard_map/pallas_call | solution.py:231
  57.5 1.1 %copy.6 = bf16[128,5120]{1,0:T(8,128)(2,1)} copy(bf16[128,5120]{1,0:T(8,128)(2,1)S(1)} %shard_map.46) | data formatting | bytes 2621440

commit v3 on v0

v3 whole, which is shorter than its diff:
```python
import jax
import jax.numpy as jnp
from jax import lax
from jax.experimental import pallas as pl
from jax.experimental.pallas import tpu as pltpu
from jax.sharding import PartitionSpec as P

MESH = pl.DeviceIdType.MESH
SLOTS = 8
WIDE = 512
XCUT = 4
EARLY = 2
OWN = 1
ORDER = (
    "d0", "d1", "d2", "c0", "d3", "c1", "d4", "c2", "c3", "d5", "p0", "c4", "d6",
    "p1", "c5", "d7", "p2", "c6", "p3", "f0", "d8", "p4", "c7", "d9", "f2", "c8",
    "p6", "c9", "p5", "f3", "p7", "f4", "p8", "f1", "p9", "f6", "f5", "f7", "w3",
    "f8", "f9", "w4", "w6", "w0", "w1", "w5", "w2", "w7", "w8", "w9",
)


def kernel(x, wg, wu, wd, y, xs, h, slots, acc, dsend, drecv, s1, r1, s2, r2, wsem, xsem, rsem, out_sem):
    rows, d = x.shape
    half = wg.shape[1] // 2
    unit = WIDE // 2
    first = half % unit
    steps = half // unit + 1
    chunks = d // WIDE
    part_rows = rows // 4
    top = part_rows // 2

    dp, tp = lax.axis_index("dp"), lax.axis_index("tp")
    core = lax.rem(dp, 2)
    other = {"dp": dp + 1 - 2 * core}
    right_at, left_at, far_at = lax.rem(tp + 1, 4), lax.rem(tp + 3, 4), lax.rem(tp + 2, 4)
    sides = ({"tp": right_at}, {"tp": left_at})
    to_at, from_at = (right_at, left_at), (left_at, right_at)
    base = core * half

    def gate_up(step, width):
        slot = lax.rem(step, SLOTS)
        at = base if width == first else base + first + (step - 1) * unit
        cols = pl.ds(pl.multiple_of(at, 128), width)
        for k, w in enumerate((wg, wu)):
            pltpu.make_async_copy(w.at[:, cols], slots.at[slot, :, pl.ds(k * width, width)], wsem.at[slot]).start()

    def arrive(step, width):
        slot = lax.rem(step, SLOTS)
        both = slots.at[slot, :, pl.ds(0, 2 * width)]
        pltpu.make_async_copy(both, both, wsem.at[slot]).wait()

    def down(chunk):
        slot = lax.rem(chunk + steps, SLOTS)
        cols = pl.ds(pl.multiple_of(chunk * WIDE, 128), WIDE)
        return pltpu.make_async_copy(
            wd.at[pl.ds(pl.multiple_of(base, 128), half), cols], slots.at[slot, pl.ds(0, half), :], wsem.at[slot]
        )

    def refill(step):
        @pl.when(step < steps)
        def _():
            gate_up(step, unit)

        @pl.when(jnp.logical_and(step >= steps, step < steps + chunks))
        def _():
            down(step - steps).start()

    xw = d // XCUT
    ours, theirs, everyone = pl.ds(0, rows), pl.ds(rows, rows), pl.ds(0, 2 * rows)

    def x_in(k):
        cols = pl.ds(k * xw, xw)
        return pltpu.make_async_copy(x.at[:, cols], xs.at[ours, cols], xsem.at[2 + k])

    def x_out(cols):
        return pltpu.make_async_remote_copy(
            src_ref=xs.at[ours, cols], dst_ref=xs.at[theirs, cols], send_sem=xsem.at[0], recv_sem=xsem.at[1],
            device_id=other, device_id_type=MESH,
        )

    barrier = pltpu.get_barrier_semaphore()
    for who in (other, *sides):
        pl.semaphore_signal(barrier, inc=1, device_id=who, device_id_type=MESH)
    for k in range(XCUT):
        x_in(k).start()
    gate_up(0, first)
    for k in range(XCUT):
        x_in(k).wait()
    for s in range(1, EARLY):
        gate_up(s, unit)
    pl.semaphore_wait(barrier, 3)

    for k in range(XCUT):
        x_out(pl.ds(k * xw, xw)).start()
    for s in range(EARLY, SLOTS):
        gate_up(s, unit)

    def hidden(step, width, span):
        slot = lax.rem(step, SLOTS)
        at = 0 if width == first else pl.multiple_of(first + (step - 1) * unit, 128)
        both = jnp.dot(xs[span, :], slots[slot, :, : 2 * width], preferred_element_type=jnp.float32)
        h[span, pl.ds(at, width)] = (jax.nn.silu(both[:, :width]) * both[:, width:]).astype(h.dtype)

    arrive(0, first)
    hidden(0, first, ours)

    @pl.loop(1, OWN)
    def _(s):
        arrive(s, unit)
        hidden(s, unit, ours)

    x_out(pl.ds(0, d)).wait_recv()
    hidden(0, first, theirs)
    refill(SLOTS)

    @pl.loop(1, OWN)
    def _(s):
        hidden(s, unit, theirs)
        refill(s + SLOTS)

    @pl.loop(OWN, steps)
    def _(s):
        arrive(s, unit)
        hidden(s, unit, everyone)
        refill(s + SLOTS)

    def send(src, dst, kind, j, who):
        return pltpu.make_async_remote_copy(
            src_ref=src, dst_ref=dst, send_sem=out_sem.at[kind], recv_sem=rsem.at[kind, j], device_id=who,
            device_id_type=MESH,
        )

    def cols_of(j):
        return pl.ds(j * WIDE, WIDE)

    def got(ref, kind, j):
        pltpu.make_async_copy(ref, ref, rsem.at[kind, j]).wait()

    def place(at, k=None):
        if k is None:
            return pl.ds(pl.multiple_of(at * part_rows, part_rows), part_rows)
        return pl.ds(pl.multiple_of(at * part_rows + k * top, top), top)

    def matmul(j):
        slot = (j + steps) % SLOTS
        down(j).wait()
        out = jnp.dot(h[...], slots[slot, :half, :], preferred_element_type=jnp.float32)
        acc[:, cols_of(j)] = out[:rows]
        dsend[:, cols_of(j)] = out[rows:].astype(dsend.dtype)
        send(dsend.at[:, cols_of(j)], drecv.at[:, cols_of(j)], 0, j, other).start()
        if j + SLOTS < chunks:
            down(j + SLOTS).start()

    def chip_sum(j):
        cols = cols_of(j)
        got(drecv.at[:, cols], 0, j)
        acc[:, cols] += drecv[:, cols].astype(jnp.float32)
        for k in range(2):
            s1[k, 0, :, cols] = acc[place(far_at, k), cols].astype(s1.dtype)
            s1[k, 1, :, cols] = acc[place(to_at[k], 1 - k), cols].astype(s1.dtype)
            send(s1.at[k, :, :, cols], r1.at[k, :, :, cols], 1, j, sides[k]).start()

    def second(j):
        cols = cols_of(j)
        got(r1.at[:, :, :, cols], 1, j)
        for k in range(2):
            s2[k, :, cols] = (acc[place(to_at[k], k), cols] + r1[k, 0, :, cols].astype(jnp.float32)).astype(s2.dtype)
            send(s2.at[k, :, cols], r2.at[k, :, cols], 2, j, sides[k]).start()

    def finish(j):
        cols = cols_of(j)
        got(r2.at[:, :, cols], 2, j)
        for k in range(2):
            total = acc[place(tp, k), cols] + r2[k, :, cols].astype(jnp.float32) + r1[1 - k, 1, :, cols].astype(jnp.float32)
            y[place(tp, k), cols] = total.astype(y.dtype)
        for k in range(2):
            mine = y.at[place(tp), cols]
            send(mine, mine, 3, j, sides[k]).start()

    def pass_on(j):
        cols = cols_of(j)
        got(y.at[pl.ds(0, 2 * part_rows), cols], 3, j)
        for k in range(2):
            piece = y.at[place(from_at[k], k), cols]
            send(piece, piece, 4, j, sides[k]).start()

    does = {"d": matmul, "c": chip_sum, "p": second, "f": finish, "w": pass_on}
    assert sorted(ORDER) == sorted(op + str(j) for op in does for j in range(chunks))
    for token in ORDER:
        does[token[0]](int(token[1:]))
    for j in range(chunks):
        got(y.at[pl.ds(0, part_rows), cols_of(j)], 4, j)

    x_out(pl.ds(0, d)).wait_send()
    for kind, ref in enumerate((dsend, s1, s2, y.at[pl.ds(0, 2 * part_rows), :], y.at[pl.ds(0, part_rows), :])):
        pltpu.make_async_copy(ref, ref, out_sem.at[kind]).wait()


def solution(mesh):
    assert mesh.shape["tp"] == 4 and mesh.shape["dp"] % 2 == 0

    def step(x, w_gate, w_up, w_down):
        rows, d = x.shape
        half = w_gate.shape[1] // 2
        chunks, top = d // WIDE, rows // 8
        dma = pltpu.SemaphoreType.DMA
        return pl.pallas_call(
            kernel,
            out_shape=pltpu.VMEM((rows, d), jnp.bfloat16),
            in_specs=[pl.BlockSpec(memory_space=pl.ANY)] * 4,
            out_specs=pl.BlockSpec(memory_space=pltpu.VMEM),
            scratch_shapes=[
                pltpu.VMEM((2 * rows, d), jnp.bfloat16),
                pltpu.VMEM((2 * rows, half), jnp.bfloat16),
                pltpu.VMEM((SLOTS, d, WIDE), jnp.bfloat16),
                pltpu.VMEM((rows, d), jnp.float32),
                pltpu.VMEM((rows, d), jnp.bfloat16),
                pltpu.VMEM((rows, d), jnp.bfloat16),
                pltpu.VMEM((2, 2, top, d), jnp.bfloat16),
                pltpu.VMEM((2, 2, top, d), jnp.bfloat16),
                pltpu.VMEM((2, top, d), jnp.bfloat16),
                pltpu.VMEM((2, top, d), jnp.bfloat16),
                dma((SLOTS,)),
                dma((2 + XCUT,)),
                dma((5, chunks)),
                dma((5,)),
            ],
            compiler_params=pltpu.CompilerParams(
                collective_id=0, has_side_effects=True, vmem_limit_bytes=64_000_000
            ),
        )(x, w_gate, w_up, w_down)

    return jax.shard_map(
        step,
        mesh=mesh,
        in_specs=(P("dp", None), P(None, "tp"), P(None, "tp"), P("tp", None)),
        out_specs=P("dp", None),
        check_vma=False,
    )
```

time: 133 us -> 56.2 us (0.42)
  matrix products: 72.6 us -> 0 us
  Pallas kernels: 0 us -> 55 us
  waiting for transfers between devices: 42.6 us -> 0 us
  between operations: 13.4 us -> 0.01 us
  local copies, waits for them, and re-layouts: 3.78 us -> 1.06 us
    dot_general x3 -> x0, matrix products: 72.6 us -> none  [the longest x1 24.6 us: step(): jnp.dot(hidden, w_down, preferred_element_type=jnp.float32)]
    pallas_call x0 -> x1, Pallas kernels: none -> 55 us  [step(): pl.pallas_call(kernel, out_shape=pltpu.VMEM((rows, d), jnp.bfloat16), in_...]
    psum x1 -> x0, waiting for transfers between devices: 42.5 us -> none  [step(): return lax.psum(term, 'tp')]
    unnamed x5 -> x1, local copies, waits for them, and re-layouts: 3.78 us -> 1.06 us
  transfers between devices with their start and end apart: 1 -> 0, of which waited for: 1 -> 0; matrix products, arithmetic and copies ran while one was open for 0% -> 0% of each run, Pallas kernels for 0% -> 0%
where the time goes in v3:
time: 56.2 us; the launch traced here: 56.1 us
  Pallas kernels  55 us (98%)
  local copies, waits for them, and re-layouts  1.06 us (2%)
    pallas_call x1, Pallas kernels, step(): pl.pallas_call(kernel, out_shape=pltpu.VMEM((rows, d), jnp.bfloat16), in_...  55 us

profile of v3, /device:TPU:112, one launch (start us, length us, event | category | flops | bytes accessed | tf_op | source)
XLA Modules:
  0.0 56.1 jit_solution(463325031151262876)
XLA Ops:
  0.0 55.0 %shard_map.46 = bf16[128,5120]{1,0:T(8,128)(2,1)S(1)} custom-call(bf16[128,5120]{1,0:T(8,128)(2,1)} %x.1, bf16[5120,6400]{1,0:T(8,128)(2,1)} %wg.1, bf16[5120,6400]{1,0:T(8,128)(2,1)} %wu.1, bf16[6400,5120]{1,0:T(8,128)(2,1)} %wd.1), custom_call_target="tpu_custom_call" | custom-call | tf_op jit(solution)/shard_map/pallas_call | solution.py:207
  55.0 1.1 %copy.6 = bf16[128,5120]{1,0:T(8,128)(2,1)} copy(bf16[128,5120]{1,0:T(8,128)(2,1)S(1)} %shard_map.46) | data formatting | bytes 2621440

commit v4 on v3

--- a/solution.py
+++ b/solution.py
@@ -9,13 +9,12 @@
 SLOTS = 8
 WIDE = 512
 XCUT = 4
-EARLY = 2
 OWN = 1
 ORDER = (
-    "d0", "d1", "d2", "c0", "d3", "c1", "d4", "c2", "c3", "d5", "p0", "c4", "d6",
-    "p1", "c5", "d7", "p2", "c6", "p3", "f0", "d8", "p4", "c7", "d9", "f2", "c8",
-    "p6", "c9", "p5", "f3", "p7", "f4", "p8", "f1", "p9", "f6", "f5", "f7", "w3",
-    "f8", "f9", "w4", "w6", "w0", "w1", "w5", "w2", "w7", "w8", "w9",
+    "d0", "d1", "d2", "c0", "d3", "c1", "c2", "d4", "c3", "d5", "p0", "c4", "d6",
+    "p1", "c5", "d7", "p2", "c6", "p3", "d8", "c7", "f0", "d9", "f1", "c8", "c9",
+    "p5", "p6", "f2", "p4", "p7", "f3", "p8", "p9", "f5", "f6", "f4", "f7", "f8",
+    "f9", "w3", "w0", "w5", "w4", "w2", "w1", "w7", "w8", "w6", "w9",
 )
 
 
@@ -84,15 +83,12 @@
     for k in range(XCUT):
         x_in(k).start()
     gate_up(0, first)
+    pl.semaphore_wait(barrier, 3)
+
     for k in range(XCUT):
         x_in(k).wait()
-    for s in range(1, EARLY):
-        gate_up(s, unit)
-    pl.semaphore_wait(barrier, 3)
-
-    for k in range(XCUT):
         x_out(pl.ds(k * xw, xw)).start()
-    for s in range(EARLY, SLOTS):
+    for s in range(1, SLOTS):
         gate_up(s, unit)
 
     def hidden(step, width, span):

time: 56.2 us -> 55.4 us (0.986)
  Pallas kernels: 55 us -> 54.3 us
    pallas_call x1, Pallas kernels: 55 us -> 54.3 us  [step(): pl.pallas_call(kernel, out_shape=pltpu.VMEM((rows, d), jnp.bfloat16), in_...]
where the time goes in v4:
time: 55.4 us
  Pallas kernels  54.3 us (98%)
  local copies, waits for them, and re-layouts  1.06 us (2%)
    pallas_call x1, Pallas kernels, step(): pl.pallas_call(kernel, out_shape=pltpu.VMEM((rows, d), jnp.bfloat16), in_...  54.3 us

profile of v4, /device:TPU:112, one launch (start us, length us, event | category | flops | bytes accessed | tf_op | source)
XLA Modules:
  0.0 55.4 jit_solution(9907965710131799032)
XLA Ops:
  0.0 54.3 %shard_map.46 = bf16[128,5120]{1,0:T(8,128)(2,1)S(1)} custom-call(bf16[128,5120]{1,0:T(8,128)(2,1)} %x.1, bf16[5120,6400]{1,0:T(8,128)(2,1)} %wg.1, bf16[5120,6400]{1,0:T(8,128)(2,1)} %wu.1, bf16[6400,5120]{1,0:T(8,128)(2,1)} %wd.1), custom_call_target="tpu_custom_call" | custom-call | tf_op jit(solution)/shard_map/pallas_call | solution.py:203
  54.3 1.1 %copy.6 = bf16[128,5120]{1,0:T(8,128)(2,1)} copy(bf16[128,5120]{1,0:T(8,128)(2,1)S(1)} %shard_map.46) | data formatting | bytes 2621440

commit v5 on v4

--- a/solution.py
+++ b/solution.py
@@ -11,10 +11,10 @@
 XCUT = 4
 OWN = 1
 ORDER = (
-    "d0", "d1", "d2", "c0", "d3", "c1", "c2", "d4", "c3", "d5", "p0", "c4", "d6",
-    "p1", "c5", "d7", "p2", "c6", "p3", "d8", "c7", "f0", "d9", "f1", "c8", "c9",
-    "p5", "p6", "f2", "p4", "p7", "f3", "p8", "p9", "f5", "f6", "f4", "f7", "f8",
-    "f9", "w3", "w0", "w5", "w4", "w2", "w1", "w7", "w8", "w6", "w9",
+    "d0", "d1", "c0", "d2", "c1", "d3", "c2", "d4", "c3", "p0", "d5", "c4", "p1",
+    "d6", "c5", "p2", "d7", "p3", "c6", "f0", "d8", "c7", "p4", "d9", "c8", "p5",
+    "c9", "f3", "p6", "p7", "f4", "p8", "f1", "p9", "f5", "f6", "f2", "f8", "f7",
+    "f9", "w4", "w5", "w1", "w2", "w0", "w8", "w3", "w6", "w7", "w9",
 )
 
 
@@ -82,11 +82,12 @@
         pl.semaphore_signal(barrier, inc=1, device_id=who, device_id_type=MESH)
     for k in range(XCUT):
         x_in(k).start()
+    for k in range(XCUT):
+        x_in(k).wait()
     gate_up(0, first)
     pl.semaphore_wait(barrier, 3)
 
     for k in range(XCUT):
-        x_in(k).wait()
         x_out(pl.ds(k * xw, xw)).start()
     for s in range(1, SLOTS):
         gate_up(s, unit)

time: 55.4 us -> 55.4 us (level)
  no operation moved by 1% of the time
where the time goes in v5:
time: 55.4 us; the launch traced here: 55.3 us
  Pallas kernels  54.2 us (98%)
  local copies, waits for them, and re-layouts  1.06 us (2%)
    pallas_call x1, Pallas kernels, step(): pl.pallas_call(kernel, out_shape=pltpu.VMEM((rows, d), jnp.bfloat16), in_...  54.2 us

profile of v5, /device:TPU:112, one launch (start us, length us, event | category | flops | bytes accessed | tf_op | source)
XLA Modules:
  0.0 55.3 jit_solution(1107814084009028240)
XLA Ops:
  0.0 54.2 %shard_map.46 = bf16[128,5120]{1,0:T(8,128)(2,1)S(1)} custom-call(bf16[128,5120]{1,0:T(8,128)(2,1)} %x.1, bf16[5120,6400]{1,0:T(8,128)(2,1)} %wg.1, bf16[5120,6400]{1,0:T(8,128)(2,1)} %wu.1, bf16[6400,5120]{1,0:T(8,128)(2,1)} %wd.1), custom_call_target="tpu_custom_call" | custom-call | tf_op jit(solution)/shard_map/pallas_call | solution.py:204
  54.3 1.1 %copy.6 = bf16[128,5120]{1,0:T(8,128)(2,1)} copy(bf16[128,5120]{1,0:T(8,128)(2,1)S(1)} %shard_map.46) | data formatting | bytes 2621440

commit v6 on v5

--- a/solution.py
+++ b/solution.py
@@ -154,12 +154,14 @@
         acc[:, cols] += drecv[:, cols].astype(jnp.float32)
         for k in range(2):
             s1[k, 0, :, cols] = acc[place(far_at, k), cols].astype(s1.dtype)
+            send(s1.at[k, 0, :, cols], r1.at[k, 0, :, cols], 1, j, sides[k]).start()
+        for k in range(2):
             s1[k, 1, :, cols] = acc[place(to_at[k], 1 - k), cols].astype(s1.dtype)
-            send(s1.at[k, :, :, cols], r1.at[k, :, :, cols], 1, j, sides[k]).start()
+            send(s1.at[k, 1, :, cols], r1.at[k, 1, :, cols], 5, j, sides[k]).start()
 
     def second(j):
         cols = cols_of(j)
-        got(r1.at[:, :, :, cols], 1, j)
+        got(r1.at[:, 0, :, cols], 1, j)
         for k in range(2):
             s2[k, :, cols] = (acc[place(to_at[k], k), cols] + r1[k, 0, :, cols].astype(jnp.float32)).astype(s2.dtype)
             send(s2.at[k, :, cols], r2.at[k, :, cols], 2, j, sides[k]).start()
@@ -167,6 +169,7 @@
     def finish(j):
         cols = cols_of(j)
         got(r2.at[:, :, cols], 2, j)
+        got(r1.at[:, 1, :, cols], 5, j)
         for k in range(2):
             total = acc[place(tp, k), cols] + r2[k, :, cols].astype(jnp.float32) + r1[1 - k, 1, :, cols].astype(jnp.float32)
             y[place(tp, k), cols] = total.astype(y.dtype)
@@ -189,7 +192,7 @@
         got(y.at[pl.ds(0, part_rows), cols_of(j)], 4, j)
 
     x_out(pl.ds(0, d)).wait_send()
-    for kind, ref in enumerate((dsend, s1, s2, y.at[pl.ds(0, 2 * part_rows), :], y.at[pl.ds(0, part_rows), :])):
+    for kind, ref in enumerate((dsend, s2, s2, y.at[pl.ds(0, 2 * part_rows), :], s2, s2)):
         pltpu.make_async_copy(ref, ref, out_sem.at[kind]).wait()
 
 
@@ -219,8 +222,8 @@
                 pltpu.VMEM((2, top, d), jnp.bfloat16),
                 dma((SLOTS,)),
                 dma((2 + XCUT,)),
-                dma((5, chunks)),
-                dma((5,)),
+                dma((6, chunks)),
+                dma((6,)),
             ],
             compiler_params=pltpu.CompilerParams(
                 collective_id=0, has_side_effects=True, vmem_limit_bytes=64_000_000

time: 55.4 us -> 55.7 us (level)
  no operation moved by 1% of the time
where the time goes in v6:
time: 55.7 us; the launch traced here: 55.6 us
  Pallas kernels  54.5 us (98%)
  local copies, waits for them, and re-layouts  1.06 us (2%)
    pallas_call x1, Pallas kernels, step(): pl.pallas_call(kernel, out_shape=pltpu.VMEM((rows, d), jnp.bfloat16), in_...  54.5 us

profile of v6, /device:TPU:112, one launch (start us, length us, event | category | flops | bytes accessed | tf_op | source)
XLA Modules:
  0.0 55.6 jit_solution(6328033242810091873)
XLA Ops:
  0.0 54.5 %shard_map.46 = bf16[128,5120]{1,0:T(8,128)(2,1)S(1)} custom-call(bf16[128,5120]{1,0:T(8,128)(2,1)} %x.1, bf16[5120,6400]{1,0:T(8,128)(2,1)} %wg.1, bf16[5120,6400]{1,0:T(8,128)(2,1)} %wu.1, bf16[6400,5120]{1,0:T(8,128)(2,1)} %wd.1), custom_call_target="tpu_custom_call" | custom-call | tf_op jit(solution)/shard_map/pallas_call | solution.py:207
  54.5 1.1 %copy.6 = bf16[128,5120]{1,0:T(8,128)(2,1)} copy(bf16[128,5120]{1,0:T(8,128)(2,1)S(1)} %shard_map.46) | data formatting | bytes 2621440
